TPU v7x, 32 devices: a whole 2x2x4 slice. The times are simulated.
32 devices in a mesh: row: 8 (over z, core), col: 4 (over y, x).
Axes of the slice: x: 2, y: 2, z: 4, core: 2. Of those that a mesh axis runs over, the one named last changes fastest.
Arguments:
- basis: float32 [8192, 1024], P('row', 'col'), may hold values from -6 to 6
- merge_coef: float32 [1024, 4096], P('row', 'col'), may hold values from -0.1875 to 0.1875
- panels: float32 [2, 8192, 256], P(None, ('row', 'col')), may hold values from -0.0625 to 0.0625
- factors: float32 [2, 256, 256], replicated, may hold values from -1 to 1
Outputs:
- vectors: float32 [8192, 4096], P(('row', 'col'))
- wsum: float32 [2, 256], replicated
All inputs are finite; a program needn't handle non-finite values.
Results may differ from a plain program's by a relative error of at most 0.0001.
Values sent between devices are 32-bit elements; how exact they have to be, the bound alone decides.
No kernel may reach another device: no remote copies, remote signals or barrier semaphores. Data moves between devices by JAX's collectives and lax.ppermute only.
A program may use at most 128 MiB of HBM per device.

v0:
```python
import jax
import jax.numpy as jnp
from jax import lax
from jax.sharding import PartitionSpec as P

HI = lax.Precision.HIGHEST


def matmul(left, right):
    return jnp.dot(left, right, precision=HI, preferred_element_type=jnp.float32)


def to_tall(block):
    return lax.all_to_all(block, "col", split_axis=0, concat_axis=1, tiled=True)


def per_device(basis, merge_coef, panels, factors):
    coef = lax.all_gather(merge_coef, "row", axis=0, tiled=True)
    block = matmul(lax.all_gather(basis, "col", axis=1, tiled=True), coef)
    upper = jnp.triu(factors)
    local_v = lax.all_gather(panels, "col", axis=1, tiled=True)

    def reduce_terms(terms):
        return lax.psum(terms, "row")

    field = block
    first = local_v[0]
    second = local_v[1]
    proj_one = reduce_terms(matmul(first.T, field))
    field = field - matmul(first, matmul(upper[0], proj_one))
    proj_two = reduce_terms(matmul(second.T, field))
    field = field - matmul(second, matmul(upper[1], proj_two))
    row_one = jnp.sum(proj_one, axis=1)
    row_two = jnp.sum(proj_two, axis=1)
    row_one, row_two = lax.psum((row_one, row_two), "col")
    field = to_tall(field)
    scale = jnp.sqrt(jnp.float32(field.shape[1]))
    return (field, jnp.stack([row_one, row_two]) / scale)


def solution(mesh):
    placed = (P("row", "col"), P("row", "col"), P(None, ("row", "col"), None), P())
    return jax.shard_map(
        per_device,
        mesh=mesh,
        in_specs=placed,
        out_specs=(P(("row", "col"), None), P()),
        check_vma=False,
    )
```

profile of v0, /device:TPU:0, one launch (start us, length us, event | category | flops | bytes accessed | tf_op | source)
XLA Modules:
  0.0 370.3 jit_solution(15266776425502628769)
XLA Ops:
  7.2 0.7 all-gather.4.cloned.1.call-update
  7.9 0.7 all-gather.6.cloned.1.call-update
  8.7 0.7 all-gather.8.cloned.1.call-update
  9.4 55.6 %all-gather.4.cloned.1.call-done = f32[1024,1024]{1,0:T(8,128)} async-done(((f32[1024,256]{1,0:T(8,128)}), f32[1024,1024]{1,0:T(8,128)}) %all-gather.4.cloned.1.call-update) | async-done | bytes 4194320 | tf_op jit(solution)/shard_map/all_gather | solution.py:19
  65.0 48.5 %all-gather.6.cloned.1.call-done = f32[1024,1024]{1,0:T(8,128)} async-done(((f32[128,1024]{1,0:T(8,128)}), f32[1024,1024]{1,0:T(8,128)}) %all-gather.6.cloned.1.call-update) | async-done | bytes 4194320 | tf_op jit(solution)/shard_map/all_gather | solution.py:18
  113.5 17.5 %fusion.2 = f32[1024,1024]{1,0:T(8,128)} fusion(f32[1024,1024]{1,0:T(8,128)} %all-gather.4.cloned.1.call-done, f32[1024,1024]{1,0:T(8,128)} %all-gather.6.cloned.1.call-done), kind=kOutput, calls=%fused_computation.14 | convolution fusion | flops 12884901888 | bytes 12582912 | tf_op jit(solution)/shard_map/dot_general | solution.py:10
  131.0 18.4 %all-gather.8.cloned.1.call-done = f32[2,1024,256]{2,1,0:T(8,128)} async-done(((f32[2,256,256]{2,1,0:T(8,128)}), f32[2,1024,256]{2,1,0:T(8,128)}) %all-gather.8.cloned.1.call-update) | async-done | bytes 2097168 | tf_op jit(solution)/shard_map/all_gather | solution.py:21
  149.4 10.3 %convolution_bitcast_fusion.1 = f32[256,1024]{0,1:T(8,128)} fusion(f32[1024,1024]{1,0:T(8,128)} %fusion.2, f32[2,1024,256]{2,1,0:T(8,128)} %all-gather.8.cloned.1.call-done), kind=kOutput, calls=%fused_computation.3 | convolution fusion | flops 3221225472 | bytes 6291456 | tf_op jit(solution)/shard_map/dot_general | solution.py:10
  159.8 0.1 iota_compare_fusion
  159.9 0.1 broadcast_select_fusion
  159.9 59.2 %all-reduce.4.cloned.1.call-done = f32[256,1024]{0,1:T(8,128)} async-done(((f32[256,1024]{0,1:T(8,128)}), f32[256,1024]{0,1:T(8,128)}) %all-reduce.4.cloned.1.call-update) | async-done | bytes 1048592 | tf_op jit(solution)/shard_map/psum | solution.py:24
  219.2 2.3 fusion.1
  221.4 5.7 %bitcast_subtract_fusion.1 = f32[1024,1024]{1,0:T(8,128)S(1)} fusion(f32[1024,1024]{1,0:T(8,128)} %fusion.2, f32[256,1024]{1,0:T(8,128)S(1)} %fusion.1, f32[2,1024,256]{2,1,0:T(8,128)S(1)} %copy-done.1), kind=kOutput, calls=%fused_computation.1 | convolution fusion | flops 3222274048 | bytes 10485760 | tf_op jit(solution)/shard_map/dot_general | solution.py:10
  227.1 2.0 copy-done
  229.1 7.8 %convolution_bitcast_fusion = f32[256,1024]{0,1:T(8,128)} fusion(f32[1024,1024]{1,0:T(8,128)S(1)} %bitcast_subtract_fusion.1, f32[2,1024,256]{2,1,0:T(8,128)S(1)} %copy-done.1), kind=kOutput, calls=%fused_computation.2 | convolution fusion | flops 3221225472 | bytes 6291456 | tf_op jit(solution)/shard_map/dot_general | solution.py:10
  237.0 58.5 %all-reduce.6.cloned.1.call-done = f32[256,1024]{0,1:T(8,128)} async-done(((f32[256,1024]{0,1:T(8,128)}), f32[256,1024]{0,1:T(8,128)}) %all-reduce.6.cloned.1.call-update) | async-done | bytes 1048592 | tf_op jit(solution)/shard_map/psum | solution.py:24
  295.5 2.3 fusion
  297.7 6.7 %bitcast_subtract_fusion = f32[1024,1024]{1,0:T(8,128)} fusion(f32[1024,1024]{1,0:T(8,128)} %copy-done, f32[256,1024]{1,0:T(8,128)S(1)} %fusion, f32[2,1024,256]{2,1,0:T(8,128)S(1)} %copy-done.1), kind=kOutput, calls=%fused_computation | convolution fusion | flops 3222274048 | bytes 10485760 | tf_op jit(solution)/shard_map/dot_general | solution.py:10
  304.4 5.0 %all-to-all-start = ((f32[4,256,1024]{2,1,0:T(8,128)}), f32[4,256,1024]{2,1,0:T(8,128)}, u32[]{:S(2)}, u32[]{:S(2)}) async-start(f32[4,256,1024]{2,1,0:T(8,128)} %bitcast.36), calls=%async_computation | async-start | bytes 8388608 | tf_op jit(solution)/shard_map/all_to_all | solution.py:14
  309.4 0.2 reduce_sum.18
  309.6 0.2 reduce_sum.19
  309.7 48.7 %all-reduce = (f32[1,256]{1,0:T(1,128)S(1)}, f32[1,256]{1,0:T(1,128)S(1)}) all-reduce(f32[1,256]{1,0:T(1,128)S(1)} %bitcast.39, f32[1,256]{1,0:T(1,128)S(1)} %bitcast.38), channel_id=1, replica_groups=mesh['row'=8,'col'=4] {'col'}, use_global_device_ids=true, to_apply=%region_5.6 | all-reduce | flops 512 | bytes 4096 | tf_op jit(solution)/shard_map/psum | solution.py:35
  358.4 0.6 maximum_multiply_fusion
  359.0 4.8 %copy.7 = f32[4,32,8,1024]{3,2,0,1:T(8,128)} copy(f32[4,32,8,1024]{3,2,1,0:T(8,128)} %bitcast.12) | data formatting | bytes 8388608 | tf_op jit(solution)/shard_map/all_to_all | solution.py:14
  (18 shorter events, 0.3 us)
Async XLA Ops:
  7.2 57.8 %all-gather.4.cloned.1.call-start = ((), (), s32[]{:S(2)}) async-start(), calls=%async_computation.1 | async-start | bytes 5242880 | tf_op jit(solution)/shard_map/all_gather | solution.py:19
  7.9 105.6 %all-gather.6.cloned.1.call-start = ((), (), s32[]{:S(2)}) async-start(), calls=%async_computation.2 | async-start | bytes 4718592 | tf_op jit(solution)/shard_map/all_gather | solution.py:18
  8.6 140.7 %all-gather.8.cloned.1.call-start = ((), (), s32[]{:S(2)}) async-start(), calls=%async_computation.3 | async-start | bytes 2621440 | tf_op jit(solution)/shard_map/all_gather | solution.py:21
  9.4 209.8 %all-reduce.4.cloned.1.call-start = ((), (), s32[]{:S(2)}) async-start(), calls=%async_computation.4 | async-start | bytes 2097152 | tf_op jit(solution)/shard_map/psum | solution.py:24
  131.0 28.9 %copy-start.4 = (f32[2,256,256]{2,1,0:T(8,128)S(1)}, f32[2,256,256]{2,1,0:T(8,128)}, u32[]{:S(2)}) copy-start(f32[2,256,256]{2,1,0:T(8,128)} %param.7) | copy-start | bytes 1572868
  149.4 72.1 %copy-start.1 = (f32[2,1024,256]{2,1,0:T(8,128)S(1)}, f32[2,1024,256]{2,1,0:T(8,128)}, u32[]{:S(2)}) copy-start(f32[2,1024,256]{2,1,0:T(8,128)} %all-gather.8.cloned.1.call-done) | copy-start | bytes 6291460
  159.7 135.8 %all-reduce.6.cloned.1.call-start = ((), (), s32[]{:S(2)}) async-start(), calls=%async_computation.5 | async-start | bytes 2097152 | tf_op jit(solution)/shard_map/psum | solution.py:24
  227.1 2.0 copy-start
  304.4 5.0 %copy-start.2 = (f32[256,1024]{0,1:T(8,128)S(1)}, f32[256,1024]{0,1:T(8,128)}, u32[]{:S(2)}) copy-start(f32[256,1024]{0,1:T(8,128)} %all-reduce.4.cloned.1.call-done) | copy-start | bytes 3145732
  304.4 5.1 %copy-start.3 = (f32[256,1024]{0,1:T(8,128)S(1)}, f32[256,1024]{0,1:T(8,128)}, u32[]{:S(2)}) copy-start(f32[256,1024]{0,1:T(8,128)} %all-reduce.6.cloned.1.call-done) | copy-start | bytes 3145732
  304.4 54.5 %all-to-all-start = ((f32[4,256,1024]{2,1,0:T(8,128)}), f32[4,256,1024]{2,1,0:T(8,128)}, u32[]{:S(2)}, u32[]{:S(2)}) async-start(f32[4,256,1024]{2,1,0:T(8,128)} %bitcast.36), calls=%async_computation | async-start | bytes 8388608 | tf_op jit(solution)/shard_map/all_to_all | solution.py:14
Sparse Core Ops, SparseCore 0:
  9.8 55.1 all-gather.3
  66.6 46.8 all-gather.5
  115.3 33.9 all-gather.7
  159.8 59.2 all-reduce.3
  237.1 58.2 all-reduce.5
where the time goes:
time: 371 us; the launch traced here: 370 us
  waiting for transfers between devices  242 us (65%)
  matrix products  52.5 us (14%)
  blocking collectives  48.7 us (13%)
  between operations  13.9 us (4%)
  local copies, waits for them, and re-layouts  6.81 us (2%)
  starting transfers between devices  5.16 us (1%)
    psum x2, waiting for transfers between devices, reduce_terms(): return lax.psum(terms, 'row')  118 us
    all_gather x1, waiting for transfers between devices, per_device(): block = matmul(lax.all_gather(basis, 'col', axis=1, tiled=True), coef)  55.6 us
    dot_general x7, matrix products, matmul(): jnp.dot(left, right, precision=HI, preferred_element_type=jnp.float32)  52.5 us
    psum x1, blocking collectives, per_device(): row_one, row_two = lax.psum((row_one, row_two), 'col')  48.7 us
    all_gather x1, waiting for transfers between devices, per_device(): coef = lax.all_gather(merge_coef, 'row', axis=0, tiled=True)  48.5 us
    all_gather x1, waiting for transfers between devices, per_device(): local_v = lax.all_gather(panels, 'col', axis=1, tiled=True)  18.4 us
  transfers between devices with their start and end apart: 6, of which 5 were waited for; matrix products, arithmetic and copies ran while one was open for 5% of the time, Pallas kernels for 0%

commit v1 on v0

--- a/solution.py
+++ b/solution.py
@@ -15,7 +15,12 @@
 
 
 def per_device(basis, merge_coef, panels, factors):
-    coef = lax.all_gather(merge_coef, "row", axis=0, tiled=True)
+    ring = [merge_coef]
+    for hop in range(7):
+        ring.append(lax.ppermute(ring[-1], "row", [(dev, (dev + 1) % 8) for dev in range(8)]))
+    coef = jnp.roll(
+        jnp.concatenate(ring[::-1], axis=0), (lax.axis_index("row") + 1) * ring[0].shape[0], axis=0
+    )
     block = matmul(lax.all_gather(basis, "col", axis=1, tiled=True), coef)
     upper = jnp.triu(factors)
     local_v = lax.all_gather(panels, "col", axis=1, tiled=True)

time: 371 us -> 338 us (0.911)
  waiting for transfers between devices: 242 us -> 191 us
  local copies, waits for them, and re-layouts: 6.81 us -> 24.5 us
    ppermute x0 -> x7, waiting for transfers between devices: none -> 73.9 us  [per_device(): lax.ppermute(ring[-1], 'row', [(dev, (dev + 1) % 8) for dev in range(8)])]
    all_gather x1, waiting for transfers between devices: 55.6 us -> 0.01 us  [per_device(): block = matmul(lax.all_gather(basis, 'col', axis=1, tiled=True), coef)]
    all_gather x1 -> x0, waiting for transfers between devices: 48.5 us -> none  [per_device(): coef = lax.all_gather(merge_coef, 'row', axis=0, tiled=True)]
    all_gather x1, waiting for transfers between devices: 18.4 us -> 0.01 us  [per_device(): local_v = lax.all_gather(panels, 'col', axis=1, tiled=True)]
    unnamed x10 -> x27, local copies, waits for them, and re-layouts: 2.02 us -> 18.8 us
  transfers between devices with their start and end apart: 6 -> 12, of which waited for: 5 -> 9; matrix products, arithmetic and copies ran while one was open for 5% -> 11% of each run, Pallas kernels for 0% -> 0%
where the time goes in v1:
time: 338 us
  waiting for transfers between devices  191 us (57%)
  matrix products  52.9 us (16%)
  blocking collectives  48.7 us (14%)
  local copies, waits for them, and re-layouts  24.5 us (7%)
  between operations  13.9 us (4%)
  starting transfers between devices  5.69 us (2%)
    psum x2, waiting for transfers between devices, reduce_terms(): return lax.psum(terms, 'row')  116 us
    ppermute x7, waiting for transfers between devices, per_device(): lax.ppermute(ring[-1], 'row', [(dev, (dev + 1) % 8) for dev in range(8)])  73.9 us
    dot_general x7, matrix products, matmul(): jnp.dot(left, right, precision=HI, preferred_element_type=jnp.float32)  52.9 us
    psum x1, blocking collectives, per_device(): row_one, row_two = lax.psum((row_one, row_two), 'col')  48.7 us
    unnamed x27, local copies, waits for them, and re-layouts  18.8 us
  transfers between devices with their start and end apart: 12, of which 9 were waited for; matrix products, arithmetic and copies ran while one was open for 11% of the time, Pallas kernels for 0%

profile of v1, /device:TPU:0, one launch (start us, length us, event | category | flops | bytes accessed | tf_op | source)
XLA Modules:
  0.0 337.7 jit_solution(13808988333008963320)
XLA Ops:
  8.5 11.1 %collective-permute-done = f32[128,1024]{1,0:T(8,128)S(1)} collective-permute-done((f32[128,1024]{1,0:T(8,128)}, f32[128,1024]{1,0:T(8,128)S(1)}, u32[]{:S(2)}, u32[]{:S(2)}) %collective-permute-start) | collective-permute-done | bytes 524320 | tf_op jit(solution)/shard_map/ppermute | solution.py:20
  19.6 10.4 %collective-permute-done.1 = f32[128,1024]{1,0:T(8,128)S(1)} collective-permute-done((f32[128,1024]{1,0:T(8,128)S(1)}, f32[128,1024]{1,0:T(8,128)S(1)}, u32[]{:S(2)}, u32[]{:S(2)}) %collective-permute-start.1) | collective-permute-done | bytes 524320 | tf_op jit(solution)/shard_map/ppermute | solution.py:20
  30.0 10.4 %collective-permute-done.2 = f32[128,1024]{1,0:T(8,128)S(1)} collective-permute-done((f32[128,1024]{1,0:T(8,128)S(1)}, f32[128,1024]{1,0:T(8,128)S(1)}, u32[]{:S(2)}, u32[]{:S(2)}) %collective-permute-start.2) | collective-permute-done | bytes 524320 | tf_op jit(solution)/shard_map/ppermute | solution.py:20
  40.4 10.4 %collective-permute-done.3 = f32[128,1024]{1,0:T(8,128)S(1)} collective-permute-done((f32[128,1024]{1,0:T(8,128)S(1)}, f32[128,1024]{1,0:T(8,128)S(1)}, u32[]{:S(2)}, u32[]{:S(2)}) %collective-permute-start.3) | collective-permute-done | bytes 524320 | tf_op jit(solution)/shard_map/ppermute | solution.py:20
  50.8 10.4 %collective-permute-done.4 = f32[128,1024]{1,0:T(8,128)S(1)} collective-permute-done((f32[128,1024]{1,0:T(8,128)S(1)}, f32[128,1024]{1,0:T(8,128)S(1)}, u32[]{:S(2)}, u32[]{:S(2)}) %collective-permute-start.4) | collective-permute-done | bytes 524320 | tf_op jit(solution)/shard_map/ppermute | solution.py:20
  61.3 10.4 %collective-permute-done.5 = f32[128,1024]{1,0:T(8,128)} collective-permute-done((f32[128,1024]{1,0:T(8,128)S(1)}, f32[128,1024]{1,0:T(8,128)}, u32[]{:S(2)}, u32[]{:S(2)}) %collective-permute-start.5) | collective-permute-done | bytes 524320 | tf_op jit(solution)/shard_map/ppermute | solution.py:20
  71.7 10.7 %collective-permute-done.6 = f32[128,1024]{1,0:T(8,128)} collective-permute-done((f32[128,1024]{1,0:T(8,128)}, f32[128,1024]{1,0:T(8,128)}, u32[]{:S(2)}, u32[]{:S(2)}) %collective-permute-start.6) | collective-permute-done | bytes 524320 | tf_op jit(solution)/shard_map/ppermute | solution.py:20
  82.4 1.9 constant_dynamic-update-slice_fusion.15
  84.3 1.9 constant_dynamic-update-slice_fusion.14
  91.3 1.9 constant_dynamic-update-slice_fusion.7
  93.2 1.9 constant_dynamic-update-slice_fusion.6
  100.1 17.8 %fusion = f32[1024,1024]{0,1:T(8,128)} fusion(f32[1024,1024]{1,0:T(8,128)} %all-gather.3.cloned.1.call-done, f32[2048,1024]{1,0:T(8,128)} %constant_dynamic-update-slice_fusion, s32[]{:T(128)S(6)} %select_n.18), kind=kOutput, calls=%fused_computation | convolution fusion | flops 12884901888 | bytes 12582916 | tf_op jit(solution)/shard_map/dot_general | solution.py:10
  117.9 10.3 %convolution_bitcast_fusion.1 = f32[256,1024]{0,1:T(8,128)} fusion(f32[1024,1024]{0,1:T(8,128)} %fusion, f32[2,1024,256]{2,1,0:T(8,128)} %all-gather.5.cloned.1.call-done), kind=kOutput, calls=%fused_computation.5 | convolution fusion | flops 3221225472 | bytes 6291456 | tf_op jit(solution)/shard_map/dot_general | solution.py:10
  128.4 57.9 %all-reduce.4.cloned.1.call-done = f32[256,1024]{0,1:T(8,128)} async-done(((f32[256,1024]{0,1:T(8,128)}), f32[256,1024]{0,1:T(8,128)}) %all-reduce.4.cloned.1.call-update) | async-done | bytes 1048592 | tf_op jit(solution)/shard_map/psum | solution.py:29
  186.4 2.3 fusion.3
  188.6 5.7 %convolution_subtract_fusion.1 = f32[1024,1024]{0,1:T(8,128)S(1)} fusion(f32[1024,1024]{0,1:T(8,128)} %fusion, f32[256,1024]{1,0:T(8,128)S(1)} %fusion.3, f32[2,1024,256]{2,1,0:T(8,128)S(1)} %copy-done.1), kind=kOutput, calls=%fused_computation.3 | convolution fusion | flops 3222274048 | bytes 10485760 | tf_op jit(solution)/shard_map/dot_general | solution.py:10
  194.3 2.0 copy-done
  196.3 7.8 %convolution_bitcast_fusion = f32[256,1024]{0,1:T(8,128)} fusion(f32[1024,1024]{0,1:T(8,128)S(1)} %convolution_subtract_fusion.1, f32[2,1024,256]{2,1,0:T(8,128)S(1)} %copy-done.1), kind=kOutput, calls=%fused_computation.4 | convolution fusion | flops 3221225472 | bytes 6291456 | tf_op jit(solution)/shard_map/dot_general | solution.py:10
  204.2 58.5 %all-reduce.6.cloned.1.call-done = f32[256,1024]{0,1:T(8,128)} async-done(((f32[256,1024]{0,1:T(8,128)}), f32[256,1024]{0,1:T(8,128)}) %all-reduce.6.cloned.1.call-update) | async-done | bytes 1048592 | tf_op jit(solution)/shard_map/psum | solution.py:29
  262.7 2.3 fusion.2
  265.0 6.8 %convolution_subtract_fusion = f32[1024,1024]{0,1:T(8,128)} fusion(f32[1024,1024]{0,1:T(8,128)} %copy-done, f32[256,1024]{1,0:T(8,128)S(1)} %fusion.2, f32[2,1024,256]{2,1,0:T(8,128)S(1)} %copy-done.1), kind=kOutput, calls=%fused_computation.2 | convolution fusion | flops 3222274048 | bytes 10485760 | tf_op jit(solution)/shard_map/dot_general | solution.py:10
  271.8 5.0 %all-to-all-start = ((f32[4,256,1024]{2,1,0:T(8,128)}), f32[4,256,1024]{2,1,0:T(8,128)}, u32[]{:S(2)}, u32[]{:S(2)}) async-start(f32[4,256,1024]{2,1,0:T(8,128)} %bitcast.33), calls=%async_computation | async-start | bytes 8388608 | tf_op jit(solution)/shard_map/all_to_all | solution.py:14
  277.1 48.7 %all-reduce = (f32[1,256]{1,0:T(1,128)S(1)}, f32[1,256]{1,0:T(1,128)S(1)}) all-reduce(f32[1,256]{1,0:T(1,128)S(1)} %bitcast.36, f32[1,256]{1,0:T(1,128)S(1)} %bitcast.35), channel_id=1, replica_groups=mesh['row'=8,'col'=4] {'col'}, use_global_device_ids=true, to_apply=%region_5.6 | all-reduce | flops 512 | bytes 4096 | tf_op jit(solution)/shard_map/psum | solution.py:40
  326.3 4.8 %copy.7 = f32[4,32,8,1024]{3,2,0,1:T(8,128)} copy(f32[4,32,8,1024]{3,2,1,0:T(8,128)} %bitcast.12) | data formatting | bytes 8388608 | tf_op jit(solution)/shard_map/all_to_all | solution.py:14
  (47 shorter events, 12.6 us)
Async XLA Ops:
  7.2 83.3 %copy-start.4 = (f32[128,1024]{1,0:T(8,128)S(1)}, f32[128,1024]{1,0:T(8,128)}, u32[]{:S(2)}) copy-start(f32[128,1024]{1,0:T(8,128)} %param.5) | copy-start | bytes 1572868
  7.2 92.9 %all-gather.3.cloned.1.call-start = ((), (), s32[]{:S(2)}) async-start(), calls=%async_computation.1 | async-start | bytes 5242880 | tf_op jit(solution)/shard_map/all_gather | solution.py:24
  7.9 110.0 %all-gather.5.cloned.1.call-start = ((), (), s32[]{:S(2)}) async-start(), calls=%async_computation.2 | async-start | bytes 2621440 | tf_op jit(solution)/shard_map/all_gather | solution.py:26
  8.0 11.6 %collective-permute-start = (f32[128,1024]{1,0:T(8,128)}, f32[128,1024]{1,0:T(8,128)S(1)}, u32[]{:S(2)}, u32[]{:S(2)}) collective-permute-start(f32[128,1024]{1,0:T(8,128)} %param.5), channel_id=1, source_target_pairs={{0,4},{4,8},{8,12},{12,16},{16,20},{20,24},{24,28},{28,0},{1,5},{5... | collective-permute-start | bytes 1572872 | tf_op jit(solution)/shard_map/ppermute | solution.py:20
  19.6 10.4 %collective-permute-start.1 = (f32[128,1024]{1,0:T(8,128)S(1)}, f32[128,1024]{1,0:T(8,128)S(1)}, u32[]{:S(2)}, u32[]{:S(2)}) collective-permute-start(f32[128,1024]{1,0:T(8,128)S(1)} %collective-permute-done), channel_id=1, source_target_pairs={{0,4},{4,8},{8,12},{12,16},{16,20},{20,24},{24,28},{28,0},{1,5},{5... | collective-permute-start | bytes 1572872 | tf_op jit(solution)/shard_map/ppermute | solution.py:20
  30.0 10.4 %collective-permute-start.2 = (f32[128,1024]{1,0:T(8,128)S(1)}, f32[128,1024]{1,0:T(8,128)S(1)}, u32[]{:S(2)}, u32[]{:S(2)}) collective-permute-start(f32[128,1024]{1,0:T(8,128)S(1)} %collective-permute-done.1), channel_id=1, source_target_pairs={{0,4},{4,8},{8,12},{12,16},{16,20},{20,24},{24,28},{28,0},{1,5},{5... | collective-permute-start | bytes 1572872 | tf_op jit(solution)/shard_map/ppermute | solution.py:20
  40.4 10.4 %collective-permute-start.3 = (f32[128,1024]{1,0:T(8,128)S(1)}, f32[128,1024]{1,0:T(8,128)S(1)}, u32[]{:S(2)}, u32[]{:S(2)}) collective-permute-start(f32[128,1024]{1,0:T(8,128)S(1)} %collective-permute-done.2), channel_id=1, source_target_pairs={{0,4},{4,8},{8,12},{12,16},{16,20},{20,24},{24,28},{28,0},{1,5},{5... | collective-permute-start | bytes 1572872 | tf_op jit(solution)/shard_map/ppermute | solution.py:20
  50.8 10.4 %collective-permute-start.4 = (f32[128,1024]{1,0:T(8,128)S(1)}, f32[128,1024]{1,0:T(8,128)S(1)}, u32[]{:S(2)}, u32[]{:S(2)}) collective-permute-start(f32[128,1024]{1,0:T(8,128)S(1)} %collective-permute-done.3), channel_id=1, source_target_pairs={{0,4},{4,8},{8,12},{12,16},{16,20},{20,24},{24,28},{28,0},{1,5},{5... | collective-permute-start | bytes 1572872 | tf_op jit(solution)/shard_map/ppermute | solution.py:20
  61.2 10.5 %collective-permute-start.5 = (f32[128,1024]{1,0:T(8,128)S(1)}, f32[128,1024]{1,0:T(8,128)}, u32[]{:S(2)}, u32[]{:S(2)}) collective-permute-start(f32[128,1024]{1,0:T(8,128)S(1)} %collective-permute-done.4), channel_id=1, source_target_pairs={{0,4},{4,8},{8,12},{12,16},{16,20},{20,24},{24,28},{28,0},{1,5},{5... | collective-permute-start | bytes 1572872 | tf_op jit(solution)/shard_map/ppermute | solution.py:20
  61.2 125.1 %all-reduce.4.cloned.1.call-start = ((), (), s32[]{:S(2)}) async-start(), calls=%async_computation.3 | async-start | bytes 2097152 | tf_op jit(solution)/shard_map/psum | solution.py:29
  71.7 10.7 %collective-permute-start.6 = (f32[128,1024]{1,0:T(8,128)}, f32[128,1024]{1,0:T(8,128)}, u32[]{:S(2)}, u32[]{:S(2)}) collective-permute-start(f32[128,1024]{1,0:T(8,128)} %collective-permute-done.5), channel_id=1, source_target_pairs={{0,4},{4,8},{8,12},{12,16},{16,20},{20,24},{24,28},{28,0},{1,5},{5... | collective-permute-start | bytes 1572872 | tf_op jit(solution)/shard_map/ppermute | solution.py:20
  100.1 28.3 %copy-start.5 = (f32[2,256,256]{2,1,0:T(8,128)S(1)}, f32[2,256,256]{2,1,0:T(8,128)}, u32[]{:S(2)}) copy-start(f32[2,256,256]{2,1,0:T(8,128)} %param.7) | copy-start | bytes 1572868
  117.9 70.7 %copy-start.1 = (f32[2,1024,256]{2,1,0:T(8,128)S(1)}, f32[2,1024,256]{2,1,0:T(8,128)}, u32[]{:S(2)}) copy-start(f32[2,1024,256]{2,1,0:T(8,128)} %all-gather.5.cloned.1.call-done) | copy-start | bytes 6291460
  128.2 134.6 %all-reduce.6.cloned.1.call-start = ((), (), s32[]{:S(2)}) async-start(), calls=%async_computation.4 | async-start | bytes 2097152 | tf_op jit(solution)/shard_map/psum | solution.py:29
  194.3 2.0 copy-start
  265.0 11.8 %copy-start.2 = (f32[256,1024]{0,1:T(8,128)S(1)}, f32[256,1024]{0,1:T(8,128)}, u32[]{:S(2)}) copy-start(f32[256,1024]{0,1:T(8,128)} %all-reduce.4.cloned.1.call-done) | copy-start | bytes 3145732
  271.8 5.1 %copy-start.3 = (f32[256,1024]{0,1:T(8,128)S(1)}, f32[256,1024]{0,1:T(8,128)}, u32[]{:S(2)}) copy-start(f32[256,1024]{0,1:T(8,128)} %all-reduce.6.cloned.1.call-done) | copy-start | bytes 3145732
  271.8 54.6 %all-to-all-start = ((f32[4,256,1024]{2,1,0:T(8,128)}), f32[4,256,1024]{2,1,0:T(8,128)}, u32[]{:S(2)}, u32[]{:S(2)}) async-start(f32[4,256,1024]{2,1,0:T(8,128)} %bitcast.33), calls=%async_computation | async-start | bytes 8388608 | tf_op jit(solution)/shard_map/all_to_all | solution.py:14
Sparse Core Ops, SparseCore 0:
  9.8 55.1 all-gather.2
  66.8 35.1 all-gather.4
  128.3 58.0 all-reduce.3
  204.3 58.3 all-reduce.5
